TPU v7x, 128 devices: a whole 4x4x4 slice. The times are simulated.
128 devices in a mesh: isl: 4 (over z_hi, core), fsdp: 32 (over x, z_lo, y).
Axes of the slice: x: 4, y: 4, z: 4 (z_hi: 2, z_lo: 2; z = z_hi * 2 + z_lo), core: 2. Of those that a mesh axis runs over, the one named last changes fastest.
Arguments:
- weights: float32 [3, 7168, 4096], P(None, 'fsdp', 'isl'), may hold values from -6 to 6
- momentum: float32 [3, 7168, 4096], P(None, 'fsdp', 'isl'), may hold values from -0.12 to 0.12
- first_moment: bfloat16 [4, 3, 7168, 4096], P('isl', None, 'fsdp'), may hold values from -0.00029945374 to 0.00029945374
- second_moment: bfloat16 [4, 3, 7168, 4096], P('isl', None, 'fsdp'), may hold values from 9.95351e-09 to 9.953976e-06
- inputs: bfloat16 [2, 1024, 4096], P(None, ('isl', 'fsdp')), may hold values from -6 to 6
- targets: bfloat16 [2, 1024, 4096], P(None, ('isl', 'fsdp')), may hold values from -6 to 6
- overflow_step: int32 [4, 32], P('isl', 'fsdp'), may hold values from 0 to 63
Outputs:
- new_weights: float32 [3, 7168, 4096], P(None, 'fsdp', 'isl')
- new_momentum: float32 [3, 7168, 4096], P(None, 'fsdp', 'isl')
Inputs may be any that keep to these rules, and one draw needn't show every extreme that they name: `overflow_step`: A device reports an overflow at inner step k when its value equals k; values of 2 or more report none.
All inputs are finite; a program needn't handle non-finite values.
Results may differ from a plain program's by a relative error of at most 0.004.
Values may be sent and summed in bfloat16 or wider, within the bound.
No kernel may reach another device: no remote copies, remote signals or barrier semaphores. Data moves between devices by JAX's collectives and lax.ppermute only.
A program may use at most 128 MiB of HBM per device.

v0:
```python
import math
import jax
import jax.numpy as jnp
from jax import lax
from jax.sharding import PartitionSpec as P

D = 4096
FF = 7168
inner_rate = 0.02
beta_first = 0.9
beta_second = 0.95
epsilon = 1e-08
decay_rate = 0.1
outer_rate = 0.7
nesterov_coef = 0.9


def joined_along(parts, dim):
    dims = list(parts.shape[1:])
    dims[dim] *= parts.shape[0]
    return jnp.moveaxis(parts, 0, dim).reshape(dims)


def copy_for_each(shard, axis):
    copies = jnp.broadcast_to(shard, (lax.axis_size(axis), *shard.shape))
    return lax.all_to_all(copies, axis, split_axis=0, concat_axis=0, tiled=True)


def collect(shard, axis, dim):
    return joined_along(copy_for_each(shard, axis), dim)


def taken_together(shard, axis):
    return copy_for_each(shard, axis).sum(axis=0)


def split_up(shard, dim, devices):
    before, after = (shard.shape[:dim], shard.shape[dim + 1 :])
    return jnp.moveaxis(shard.reshape(*before, devices, -1, *after), dim, 0)


def sum_at_owner(shard, axis, dim):
    devices = lax.axis_size(axis)
    parts = lax.all_to_all(split_up(shard, dim, devices), axis, 0, 0, tiled=True)
    return jnp.sum(parts, axis=0)


def silu_parts(preact):
    sigmoid_value = jax.nn.sigmoid(preact)
    return (preact * sigmoid_value, sigmoid_value * (1.0 + preact * (1.0 - sigmoid_value)))


def contract_last(left_side, right_side):
    return lax.dot_general(
        left_side, right_side, (((1,), (1,)), ((), ())), preferred_element_type=jnp.float32
    )


def contract_first(left_side, right_side):
    return lax.dot_general(
        left_side, right_side, (((0,), (0,)), ((), ())), preferred_element_type=jnp.float32
    )


def body(weights, momentum, first_moment, second_moment, inputs, targets, overflow_step):
    island_count = lax.axis_size("isl")
    gathered = collect(weights.astype(jnp.bfloat16), "isl", 2).astype(weights.dtype)
    current = gathered
    moment_one = first_moment[0].astype(jnp.float32)
    moment_two = second_moment[0].astype(jnp.float32)
    inner_count = inputs.shape[0]
    island_tokens = inputs.shape[1] * lax.axis_size("fsdp")
    overflow_marks = (overflow_step.reshape(1) == jnp.arange(inner_count, dtype=jnp.int32)).astype(
        jnp.int32
    )
    overflow_counts = taken_together(overflow_marks, "fsdp")
    all_inputs = lax.all_gather(inputs, "fsdp", axis=1, tiled=True)
    for inner_step in range(inner_count):
        rounded = current.astype(jnp.bfloat16)
        local_inputs = inputs[inner_step]
        local_targets = targets[inner_step]
        every_input = all_inputs[inner_step]
        gate_pre = contract_last(every_input, rounded[0]) / math.sqrt(D)
        up_pre = contract_last(every_input, rounded[1]) / math.sqrt(D)
        activated, slope = silu_parts(gate_pre)
        hidden = (activated * up_pre).astype(jnp.bfloat16)
        partial_value = jnp.dot(hidden, rounded[2], preferred_element_type=jnp.float32)
        summed = sum_at_owner(partial_value, "fsdp", 0)
        outputs = local_inputs.astype(jnp.float32) + summed / math.sqrt(FF)
        own_slopes = ((outputs - local_targets.astype(jnp.float32)) / island_tokens).astype(
            jnp.bfloat16
        )
        slopes = collect(own_slopes, "fsdp", 0)
        hidden_slope = contract_last(slopes, rounded[2]) / math.sqrt(FF)
        gate_slope = (hidden_slope * up_pre * slope).astype(jnp.bfloat16)
        up_slope = (hidden_slope * activated).astype(jnp.bfloat16)
        grad_gate = contract_first(gate_slope, every_input) / math.sqrt(D)
        grad_up = contract_first(up_slope, every_input) / math.sqrt(D)
        grad_down = contract_first(hidden, slopes) / math.sqrt(FF)
        gradient = jnp.stack([grad_gate, grad_up, grad_down])
        overflow_count = overflow_counts[inner_step]
        skipped = overflow_count > 0
        next_one = beta_first * moment_one + (1.0 - beta_first) * gradient
        next_two = beta_second * moment_two + (1.0 - beta_second) * gradient * gradient
        next_weights = current - inner_rate * (
            next_one / (jnp.sqrt(next_two) + epsilon) + decay_rate * current
        )
        current = jnp.where(skipped, current, next_weights)
        moment_one = jnp.where(skipped, moment_one, next_one)
        moment_two = jnp.where(skipped, moment_two, next_two)
    pseudo_term = gathered - current
    pseudo_sum = lax.psum_scatter(
        pseudo_term.astype(jnp.bfloat16), "isl", scatter_dimension=2, tiled=True
    ).astype(jnp.float32)
    outer_delta = pseudo_sum / island_count
    new_momentum = nesterov_coef * momentum + outer_delta
    new_weights = weights - outer_rate * (outer_delta + nesterov_coef * new_momentum)
    return (new_weights, new_momentum)


def solution(mesh):
    in_specs = (
        P(None, "fsdp", "isl"),
        P(None, "fsdp", "isl"),
        P("isl", None, "fsdp", None),
        P("isl", None, "fsdp", None),
        P(None, ("isl", "fsdp"), None),
        P(None, ("isl", "fsdp"), None),
        P("isl", "fsdp"),
    )
    out_specs = (P(None, "fsdp", "isl"), P(None, "fsdp", "isl"))
    return jax.shard_map(body, mesh=mesh, in_specs=in_specs, out_specs=out_specs, check_vma=False)
```

profile of v0, /device:TPU:1, one launch (start us, length us, event | category | flops | bytes accessed | tf_op | source)
XLA Modules:
  0.0 474.0 jit_solution(12137875566399298339)
XLA Ops:
  7.2 0.7 all-gather.2.cloned.1.call-update
  7.9 2.0 convert_element_type.82
  9.9 0.7 broadcast_in_dim.12
  10.6 96.8 %all_to_all.31 = bf16[4,3,224,1024]{3,2,1,0:T(8,128)(2,1)S(1)} all-to-all(bf16[4,3,224,1024]{3,2,1,0:T(8,128)(2,1)S(1)} %broadcast_in_dim.12), channel_id=1, replica_groups=mesh['isl'=4,'fsdp'=32] {'isl'}, dimensions={0} | all-to-all | bytes 11010048 | tf_op jit(solution)/shard_map/all_to_all | solution.py:26
  107.4 2.9 fusion.66
  110.9 1.4 copy.34
  112.4 2.3 reshape.54
  114.6 3.1 copy.32
  117.7 1.9 copy.41
  119.6 1.4 copy.31
  121.0 2.0 copy.40
  123.0 26.2 %all-gather.2.cloned.1.call-done = bf16[2,256,4096]{2,1,0:T(8,128)(2,1)} async-done(((bf16[2,8,4096]{2,1,0:T(8,128)(2,1)}), bf16[2,256,4096]{2,1,0:T(8,128)(2,1)}) %all-gather.2.cloned.1.call-update) | async-done | bytes 4194320 | tf_op jit(solution)/shard_map/all_gather | solution.py:77
  149.2 3.1 fusion.34
  152.6 3.1 multiply_convert_fusion.5
  155.8 4.2 fusion.55
  160.0 6.8 %all-to-all-start.2 = ((f32[32,8,4096]{2,1,0:T(8,128)}), f32[32,8,4096]{2,1,0:T(8,128)}, u32[]{:S(2)}, u32[]{:S(2)}) async-start(f32[32,8,4096]{2,1,0:T(8,128)} %fusion.55), calls=%async_computation.2 | async-start | bytes 8388608 | tf_op jit(solution)/shard_map/all_to_all | solution.py:44
  167.5 34.9 %all-to-all-done.2 = f32[32,8,4096]{2,1,0:T(8,128)} async-done(((f32[32,8,4096]{2,1,0:T(8,128)}), f32[32,8,4096]{2,1,0:T(8,128)}, u32[]{:S(2)}, u32[]{:S(2)}) %all-to-all-start.2) | async-done | bytes 4194336 | tf_op jit(solution)/shard_map/all_to_all | solution.py:44
  203.0 9.3 %all-to-all-start.1 = ((s32[32,1,2]{2,1,0:T(1,128)}), s32[32,1,2]{2,1,0:T(1,128)S(1)}, u32[]{:S(2)}, u32[]{:S(2)}) async-start(s32[32,1,2]{2,1,0:T(1,128)} %broadcast_in_dim.13), calls=%async_computation.1 | async-start | bytes 32768 | tf_op jit(solution)/shard_map/all_to_all | solution.py:26
  212.3 2.4 reduce_sum.28
  214.8 5.1 %all-to-all-done.1 = s32[32,1,2]{2,1,0:T(1,128)S(1)} async-done(((s32[32,1,2]{2,1,0:T(1,128)}), s32[32,1,2]{2,1,0:T(1,128)S(1)}, u32[]{:S(2)}, u32[]{:S(2)}) %all-to-all-start.1) | async-done | bytes 288 | tf_op jit(solution)/shard_map/all_to_all | solution.py:26
  219.9 1.6 broadcast_in_dim.14
  221.5 4.9 %all-to-all-start.3 = ((bf16[32,8,4096]{2,1,0:T(8,128)(2,1)}), bf16[32,8,4096]{2,1,0:T(8,128)(2,1)}, u32[]{:S(2)}, u32[]{:S(2)}) async-start(bf16[32,8,4096]{2,1,0:T(8,128)(2,1)} %broadcast_in_dim.14), calls=%async_computation.3 | async-start | bytes 4194304 | tf_op jit(solution)/shard_map/all_to_all | solution.py:26
  227.7 2.0 copy.42
  229.6 3.9 convert_bitcast_fusion
  233.6 6.5 %copy.39 = f32[4,3,28,8,1024]{4,3,0,2,1:T(8,128)} copy(f32[4,3,28,8,1024]{4,3,2,1,0:T(8,128)S(1)} %convert_bitcast_fusion) | data formatting | bytes 22020096 | tf_op jit(solution)/shard_map/convert_element_type | solution.py:67
  240.1 3.6 all-to-all-done.3
  243.7 2.5 fusion.16
  246.2 4.4 fusion.36
  250.6 0.7 fusion.17
  251.3 0.7 fusion.18
  252.3 2.5 slice-done.2
  254.9 1.2 slice-done.7
  256.1 11.3 %fusion.65 = bf16[3,224,4096]{2,1,0:T(8,128)(2,1)} fusion(f32[3,224,4096]{2,1,0:T(8,128)S(1)} %bitcast.142, bf16[1,3,224,4096]{3,2,1,0:T(8,128)(2,1)S(1)} %bitcast.148, f32[1,224,4096]{2,1,0:T(8,128)S(1)} %fusion.16, f32[1,224,4096]{2,1,0:T(8,128)S(1)} %fusion.17, f32[1,224,4096]{2,1,0:T(8,128)S(1)} %fusion.18, bf16[1,3,224,4096]{3,2,1,0:T(8,128)(2,1)} %param.9, ...), kind=kLoop, calls=%fused_computation.94 | loop fusion | flops 52297728 | bytes 38535168 | tf_op jit(solution)/shard_map/convert_element_type | solution.py:79
  267.4 2.4 fusion.40
  269.8 2.4 multiply_convert_fusion.2
  272.3 2.2 fusion.27
  274.5 32.4 %all_to_all.32 = f32[32,8,4096]{2,1,0:T(8,128)} all-to-all(f32[32,8,4096]{2,1,0:T(8,128)S(1)} %fusion.27), channel_id=1, replica_groups=mesh['isl'=4,'fsdp'=32] {'fsdp'}, dimensions={0} | all-to-all | bytes 8388608 | tf_op jit(solution)/shard_map/all_to_all | solution.py:44
  306.9 2.4 reduce_sum.29
  309.4 1.6 broadcast_in_dim.15
  311.0 4.0 all-to-all-start.5
  315.8 26.2 %all-to-all-done.5 = bf16[32,8,4096]{2,1,0:T(8,128)(2,1)S(1)} async-done(((bf16[32,8,4096]{2,1,0:T(8,128)(2,1)}), bf16[32,8,4096]{2,1,0:T(8,128)(2,1)S(1)}, u32[]{:S(2)}, u32[]{:S(2)}) %all-to-all-start.5) | async-done | bytes 2097184 | tf_op jit(solution)/shard_map/all_to_all | solution.py:26
  342.1 2.4 fusion.43
  344.5 2.5 fusion.13
  347.1 5.0 %fusion.14 = f32[1,224,4096]{2,1,0:T(8,128)} fusion(bf16[2,256,4096]{2,1,0:T(8,128)(2,1)} %all-gather.2.cloned.1.call-done, f32[256,224]{0,1:T(8,128)S(1)} %fusion.43, f32[256,224]{0,1:T(8,128)S(1)} %fusion.40), kind=kOutput, calls=%fused_computation.27 | convolution fusion | flops 471023616 | bytes 6225920 | tf_op jit(solution)/shard_map/dot_general | solution.py:60
  352.0 2.5 fusion.15
  354.8 20.5 %fusion.12 = bf16[3,224,4096]{2,1,0:T(8,128)(2,1)} fusion(f32[3,224,4096]{2,1,0:T(8,128)S(1)} %bitcast.145, f32[1,224,4096]{2,1,0:T(8,128)} %fusion.13, f32[1,224,4096]{2,1,0:T(8,128)} %fusion.14, f32[1,224,4096]{2,1,0:T(8,128)S(1)} %fusion.15, f32[1,224,4096]{2,1,0:T(8,128)S(1)} %copy-done.4, f32[1,224,4096]{2,1,0:T(8,128)S(1)} %copy-done.6, ...), kind=kLoop, calls=%fused_computation.23 | loop fusion | flops 104595456 | bytes 49545216 | tf_op jit(solution)/shard_map/convert_element_type | solution.py:113
  375.4 86.1 %reduce-scatter.2.cloned.1.call-done = bf16[3,224,1024]{2,1,0:T(8,128)(2,1)} async-done(((bf16[3,224,4096]{2,1,0:T(8,128)(2,1)}), bf16[3,224,1024]{2,1,0:T(8,128)(2,1)}) %reduce-scatter.2.cloned.1.call-update) | async-done | bytes 1376272 | tf_op jit(solution)/shard_map/reduce_scatter | solution.py:112
  461.4 5.7 %multiply_subtract_fusion = (f32[3,224,1024]{2,1,0:T(8,128)}, f32[3,224,1024]{2,1,0:T(8,128)}) fusion(f32[3,224,1024]{2,1,0:T(8,128)S(1)} %copy-done.9, bf16[3,224,1024]{2,1,0:T(8,128)(2,1)} %reduce-scatter.2.cloned.1.call-done, f32[3,224,1024]{2,1,0:T(8,128)} %param.8), kind=kLoop, calls=%fused_computation.36 | loop fusion | flops 5505024 | bytes 12386304 | tf_op jit(solution)/shard_map/sub | solution.py:117
  (64 shorter events, 3.3 us)
Async XLA Ops:
  7.2 142.1 %all-gather.2.cloned.1.call-start = ((), (), s32[]{:S(2)}) async-start(), calls=%async_computation.7 | async-start | bytes 4325376 | tf_op jit(solution)/shard_map/all_gather | solution.py:77
  107.4 3.5 copy-start
  114.6 5.0 %copy-start.11 = (bf16[1,224,4,1024]{3,1,0,2:T(8,128)(2,1)S(1)}, bf16[1,224,4,1024]{3,1,0,2:T(8,128)(2,1)}, u32[]{:S(2)}) copy-start(bf16[1,224,4,1024]{3,1,0,2:T(8,128)(2,1)} %get-tuple-element.6) | copy-start | bytes 5505028
  149.2 3.4 copy-start.7
  155.7 4.3 copy-start.12
  160.0 42.4 %all-to-all-start.2 = ((f32[32,8,4096]{2,1,0:T(8,128)}), f32[32,8,4096]{2,1,0:T(8,128)}, u32[]{:S(2)}, u32[]{:S(2)}) async-start(f32[32,8,4096]{2,1,0:T(8,128)} %fusion.55), calls=%async_computation.2 | async-start | bytes 8388608 | tf_op jit(solution)/shard_map/all_to_all | solution.py:44
  166.8 48.0 %copy-start.13 = (bf16[2,8,4096]{2,1,0:T(8,128)(2,1)S(1)}, bf16[2,8,4096]{2,1,0:T(8,128)(2,1)}, u32[]{:S(2)}) copy-start(bf16[2,8,4096]{2,1,0:T(8,128)(2,1)} %param.11) | copy-start | bytes 393220
  166.8 47.9 %copy-start.16 = (bf16[2,8,4096]{2,1,0:T(8,128)(2,1)S(1)}, bf16[2,8,4096]{2,1,0:T(8,128)(2,1)}, u32[]{:S(2)}) copy-start(bf16[2,8,4096]{2,1,0:T(8,128)(2,1)} %param.12) | copy-start | bytes 393220
  203.0 16.9 %all-to-all-start.1 = ((s32[32,1,2]{2,1,0:T(1,128)}), s32[32,1,2]{2,1,0:T(1,128)S(1)}, u32[]{:S(2)}, u32[]{:S(2)}) async-start(s32[32,1,2]{2,1,0:T(1,128)} %broadcast_in_dim.13), calls=%async_computation.1 | async-start | bytes 32768 | tf_op jit(solution)/shard_map/all_to_all | solution.py:26
  221.5 22.2 %all-to-all-start.3 = ((bf16[32,8,4096]{2,1,0:T(8,128)(2,1)}), bf16[32,8,4096]{2,1,0:T(8,128)(2,1)}, u32[]{:S(2)}, u32[]{:S(2)}) async-start(bf16[32,8,4096]{2,1,0:T(8,128)(2,1)} %broadcast_in_dim.14), calls=%async_computation.3 | async-start | bytes 4194304 | tf_op jit(solution)/shard_map/all_to_all | solution.py:26
  233.5 12.6 %copy-start.10 = (bf16[28,8,4,1024]{3,1,2,0:T(8,128)(2,1)S(1)}, bf16[28,8,4,1024]{3,1,2,0:T(8,128)(2,1)}, u32[]{:S(2)}) copy-start(bf16[28,8,4,1024]{3,1,2,0:T(8,128)(2,1)} %copy.42) | copy-start | bytes 5505028
  243.7 7.0 %copy-start.8 = (bf16[2,256,4096]{2,1,0:T(8,128)(2,1)S(1)}, bf16[2,256,4096]{2,1,0:T(8,128)(2,1)}, u32[]{:S(2)}) copy-start(bf16[2,256,4096]{2,1,0:T(8,128)(2,1)} %all-gather.2.cloned.1.call-done) | copy-start | bytes 12582916
  243.7 8.4 %slice-start = ((s8[11010048]{0:T(1024)(128)(4,1)}), s8[4194304]{0:T(1024)(128)(4,1)S(1)}, s32[]{:S(2)}) async-start(s8[11010048]{0:T(1024)(128)(4,1)} %bitcast.140), calls=%async_computation.9 | async-start | bytes 8388608
  246.1 6.0 %copy-start.3 = (f32[1,224,4096]{2,1,0:T(8,128)}, f32[1,224,4096]{2,1,0:T(8,128)S(1)}, u32[]{:S(2)}) copy-start(f32[1,224,4096]{2,1,0:T(8,128)S(1)} %fusion.16) | copy-start | bytes 11010052
  246.1 5.2 %copy-start.15 = (f32[256,224]{0,1:T(8,128)S(1)}, f32[256,224]{0,1:T(8,128)}, u32[]{:S(2)}) copy-start(f32[256,224]{0,1:T(8,128)} %get-tuple-element.10) | copy-start | bytes 688132
  246.2 5.9 %slice-start.1 = ((s8[11010048]{0:T(1024)(128)(4,1)}), s8[4194304]{0:T(1024)(128)(4,1)S(1)}, s32[]{:S(2)}) async-start(s8[11010048]{0:T(1024)(128)(4,1)} %bitcast.140), calls=%async_computation.10 | async-start | bytes 8388608
  246.2 6.2 %slice-start.6 = ((s8[5505024]{0:T(1024)(128)(4,1)}), s8[4194304]{0:T(1024)(128)(4,1)S(1)}, s32[]{:S(2)}) async-start(s8[5505024]{0:T(1024)(128)(4,1)} %bitcast.147), calls=%async_computation.15 | async-start | bytes 8388608
  250.6 4.2 slice-start.2
  250.6 5.5 %slice-start.7 = ((s8[5505024]{0:T(1024)(128)(4,1)}), s8[1310720]{0:T(1024)(128)(4,1)S(1)}, s32[]{:S(2)}) async-start(s8[5505024]{0:T(1024)(128)(4,1)} %bitcast.147), calls=%async_computation.16 | async-start | bytes 2621440
  251.3 16.1 %copy-start.5 = (f32[1,224,4096]{2,1,0:T(8,128)}, f32[1,224,4096]{2,1,0:T(8,128)S(1)}, u32[]{:S(2)}) copy-start(f32[1,224,4096]{2,1,0:T(8,128)S(1)} %fusion.17) | copy-start | bytes 11010052
  252.1 15.3 %copy-start.1 = (f32[1,224,4096]{2,1,0:T(8,128)}, f32[1,224,4096]{2,1,0:T(8,128)S(1)}, u32[]{:S(2)}) copy-start(f32[1,224,4096]{2,1,0:T(8,128)S(1)} %fusion.18) | copy-start | bytes 11010052
  306.9 2.4 copy-start.14
  306.9 2.5 copy-start.17
  311.0 31.1 %all-to-all-start.5 = ((bf16[32,8,4096]{2,1,0:T(8,128)(2,1)}), bf16[32,8,4096]{2,1,0:T(8,128)(2,1)S(1)}, u32[]{:S(2)}, u32[]{:S(2)}) async-start(bf16[32,8,4096]{2,1,0:T(8,128)(2,1)} %broadcast_in_dim.15), calls=%async_computation.5 | async-start | bytes 4194304 | tf_op jit(solution)/shard_map/all_to_all | solution.py:26
  315.0 146.4 %reduce-scatter.2.cloned.1.call-start = ((), (), s32[]{:S(2)}) async-start(), calls=%async_computation.8 | async-start | bytes 6881280 | tf_op jit(solution)/shard_map/reduce_scatter | solution.py:112
  342.0 12.5 %slice-start.3 = ((s8[11010048]{0:T(1024)(128)(4,1)}), s8[4194304]{0:T(1024)(128)(4,1)S(1)}, s32[]{:S(2)}) async-start(s8[11010048]{0:T(1024)(128)(4,1)} %bitcast.143), calls=%async_computation.12 | async-start | bytes 8388608
  344.5 10.0 %slice-start.4 = ((s8[11010048]{0:T(1024)(128)(4,1)}), s8[4194304]{0:T(1024)(128)(4,1)S(1)}, s32[]{:S(2)}) async-start(s8[11010048]{0:T(1024)(128)(4,1)} %bitcast.143), calls=%async_computation.13 | async-start | bytes 8388608
  344.5 10.0 %copy-start.6 = (f32[1,224,4096]{2,1,0:T(8,128)S(1)}, f32[1,224,4096]{2,1,0:T(8,128)}, u32[]{:S(2)}) copy-start(f32[1,224,4096]{2,1,0:T(8,128)} %copy-done.5) | copy-start | bytes 11010052
  347.1 7.5 %slice-start.5 = ((s8[11010048]{0:T(1024)(128)(4,1)}), s8[2621440]{0:T(1024)(128)(4,1)S(1)}, s32[]{:S(2)}) async-start(s8[11010048]{0:T(1024)(128)(4,1)} %bitcast.143), calls=%async_computation.14 | async-start | bytes 5242880
  347.1 7.5 %copy-start.4 = (f32[1,224,4096]{2,1,0:T(8,128)S(1)}, f32[1,224,4096]{2,1,0:T(8,128)}, u32[]{:S(2)}) copy-start(f32[1,224,4096]{2,1,0:T(8,128)} %copy-done.3) | copy-start | bytes 11010052
  352.0 2.8 copy-start.2
  375.3 86.1 %copy-start.9 = (f32[3,224,1024]{2,1,0:T(8,128)S(1)}, f32[3,224,1024]{2,1,0:T(8,128)}, u32[]{:S(2)}) copy-start(f32[3,224,1024]{2,1,0:T(8,128)} %param.7) | copy-start | bytes 8257540
Sparse Core Ops, SparseCore 0:
  9.6 139.5 all-gather.1
  375.5 85.9 reduce-scatter.1
where the time goes:
time: 475 us; the launch traced here: 474 us
  waiting for transfers between devices  183 us (39%)
  blocking collectives  129 us (27%)
  other arithmetic  48.3 us (10%)
  matrix products  38.1 us (8%)
  local copies, waits for them, and re-layouts  33.9 us (7%)
  starting transfers between devices  25.4 us (5%)
  between operations  16.4 us (3%)
    all_to_all x1, blocking collectives, copy_for_each(): return lax.all_to_all(copies, axis, split_axis=0, concat_axis=0, tiled=True)  96.8 us
    reduce_scatter x1, waiting for transfers between devices, body(): lax.psum_scatter(pseudo_term.astype(jnp.bfloat16), 'isl', scatter_dimensi...  86.1 us
    all_to_all x3, waiting for transfers between devices, copy_for_each(): return lax.all_to_all(copies, axis, split_axis=0, concat_axis=0, tiled=True)  34.9 us
    all_to_all x1, waiting for transfers between devices, sum_at_owner(): lax.all_to_all(split_up(shard, dim, devices), axis, 0, 0, tiled=True)  34.9 us
    all_to_all x1, blocking collectives, sum_at_owner(): lax.all_to_all(split_up(shard, dim, devices), axis, 0, 0, tiled=True)  32.4 us
    all_gather x1, waiting for transfers between devices, body(): all_inputs = lax.all_gather(inputs, 'fsdp', axis=1, tiled=True)  26.2 us
    convert_element_type x1, other arithmetic, body(): pseudo_term.astype(jnp.bfloat16)  20.5 us
    all_to_all x3, starting transfers between devices, copy_for_each(): return lax.all_to_all(copies, axis, split_axis=0, concat_axis=0, tiled=True)  18.3 us
  transfers between devices with their start and end apart: 6, of which 6 were waited for; matrix products, arithmetic and copies ran while one was open for 7% of the time, Pallas kernels for 0%

commit v1 on v0

--- a/solution.py
+++ b/solution.py
@@ -74,7 +74,9 @@
         jnp.int32
     )
     overflow_counts = taken_together(overflow_marks, "fsdp")
-    all_inputs = lax.all_gather(inputs, "fsdp", axis=1, tiled=True)
+    all_inputs = jnp.concatenate(
+        lax.all_to_all(jnp.stack([inputs] * lax.axis_size("fsdp")), "fsdp", 0, 0), axis=1
+    )
     for inner_step in range(inner_count):
         rounded = current.astype(jnp.bfloat16)
         local_inputs = inputs[inner_step]

time: 475 us -> 499 us (1.051)
  starting transfers between devices: 25.4 us -> 39.1 us
  waiting for transfers between devices: 183 us -> 195 us
  blocking collectives: 129 us -> 122 us
  matrix products: 38.1 us -> 43.4 us
    all_to_all x0 -> x1, waiting for transfers between devices: none -> 39.9 us  [body(): lax.all_to_all(jnp.stack([inputs] * lax.axis_size('fsdp')), 'fsdp', 0, 0)]
    all_to_all x1, blocking collectives: 96.8 us -> 69.3 us  [copy_for_each(): return lax.all_to_all(copies, axis, split_axis=0, concat_axis=0, tiled=True)]
    all_gather x1 -> x0, waiting for transfers between devices: 26.2 us -> none  [body(): all_inputs = lax.all_gather(inputs, 'fsdp', axis=1, tiled=True)]
    reduce_scatter x1, waiting for transfers between devices: 86.1 us -> 63.1 us  [body(): lax.psum_scatter(pseudo_term.astype(jnp.bfloat16), 'isl', scatter_dimensi...]
    all_to_all x1, blocking collectives: 32.4 us -> 52.3 us  [sum_at_owner(): lax.all_to_all(split_up(shard, dim, devices), axis, 0, 0, tiled=True)]
    all_to_all x1, waiting for transfers between devices: 34.9 us -> 50.4 us  [sum_at_owner(): lax.all_to_all(split_up(shard, dim, devices), axis, 0, 0, tiled=True)]
    all_to_all x0 -> x1, starting transfers between devices: none -> 7.62 us  [body(): lax.all_to_all(jnp.stack([inputs] * lax.axis_size('fsdp')), 'fsdp', 0, 0)]
    all_to_all x3, waiting for transfers between devices: 34.9 us -> 41.5 us  [copy_for_each(): return lax.all_to_all(copies, axis, split_axis=0, concat_axis=0, tiled=True)]
where the time goes in v1:
time: 499 us; the launch traced here: 498 us
  waiting for transfers between devices  195 us (39%)
  blocking collectives  122 us (24%)
  other arithmetic  48.1 us (10%)
  matrix products  43.4 us (9%)
  starting transfers between devices  39.1 us (8%)
  local copies, waits for them, and re-layouts  34.1 us (7%)
  between operations  16.5 us (3%)
    all_to_all x1, blocking collectives, copy_for_each(): return lax.all_to_all(copies, axis, split_axis=0, concat_axis=0, tiled=True)  69.3 us
    reduce_scatter x1, waiting for transfers between devices, body(): lax.psum_scatter(pseudo_term.astype(jnp.bfloat16), 'isl', scatter_dimensi...  63.1 us
    all_to_all x1, blocking collectives, sum_at_owner(): lax.all_to_all(split_up(shard, dim, devices), axis, 0, 0, tiled=True)  52.3 us
    all_to_all x1, waiting for transfers between devices, sum_at_owner(): lax.all_to_all(split_up(shard, dim, devices), axis, 0, 0, tiled=True)  50.4 us
    all_to_all x3, waiting for transfers between devices, copy_for_each(): return lax.all_to_all(copies, axis, split_axis=0, concat_axis=0, tiled=True)  41.5 us
    all_to_all x1, waiting for transfers between devices, body(): lax.all_to_all(jnp.stack([inputs] * lax.axis_size('fsdp')), 'fsdp', 0, 0)  39.9 us
    all_to_all x3, starting transfers between devices, copy_for_each(): return lax.all_to_all(copies, axis, split_axis=0, concat_axis=0, tiled=True)  23.7 us
    convert_element_type x1, other arithmetic, body(): pseudo_term.astype(jnp.bfloat16)  20.4 us
  transfers between devices with their start and end apart: 6, of which 6 were waited for; matrix products, arithmetic and copies ran while one was open for 7% of the time, Pallas kernels for 0%

profile of v1, /device:TPU:1, one launch (start us, length us, event | category | flops | bytes accessed | tf_op | source)
XLA Modules:
  0.0 497.7 jit_solution(10932192148129667895)
XLA Ops:
  7.2 2.0 convert_element_type.82
  9.1 0.7 broadcast_in_dim.12
  9.9 69.3 %all_to_all.36 = bf16[4,3,224,1024]{3,2,1,0:T(8,128)(2,1)} all-to-all(bf16[4,3,224,1024]{3,2,1,0:T(8,128)(2,1)S(1)} %broadcast_in_dim.12), channel_id=1, replica_groups=mesh['isl'=4,'fsdp'=32] {'isl'}, dimensions={0} | all-to-all | bytes 11010048 | tf_op jit(solution)/shard_map/all_to_all | solution.py:26
  79.2 2.5 stack.18
  81.8 7.6 %all-to-all-start.2 = ((bf16[32,2,8,4096]{3,2,1,0:T(8,128)(2,1)}), bf16[32,2,8,4096]{3,2,1,0:T(8,128)(2,1)}, u32[]{:S(2)}, u32[]{:S(2)}) async-start(bf16[32,2,8,4096]{3,2,1,0:T(8,128)(2,1)} %stack.18), calls=%async_computation.2 | async-start | bytes 8388608 | tf_op jit(solution)/shard_map/all_to_all | solution.py:78
  89.4 5.1 %fusion.66 = (bf16[1,224,4,1024]{3,1,0,2:T(8,128)(2,1)S(1)}, bf16[1,224,4,1024]{3,1,0,2:T(8,128)(2,1)}, bf16[1,224,4,1024]{3,1,0,2:T(8,128)(2,1)}) fusion(bf16[3,224,4,1024]{3,1,0,2:T(8,128)(2,1)} %bitcast.147), kind=kLoop, calls=%fused_computation.95 | loop fusion | bytes 11010048 | tf_op jit(solution)/shard_map/slice | solution.py:89
  94.5 1.4 copy.34
  95.9 2.3 reshape.65
  98.2 3.1 copy.32
  101.2 2.0 copy.41
  103.3 1.4 copy.31
  104.7 2.0 copy.40
  106.6 39.9 %all-to-all-done.2 = bf16[32,2,8,4096]{3,2,1,0:T(8,128)(2,1)} async-done(((bf16[32,2,8,4096]{3,2,1,0:T(8,128)(2,1)}), bf16[32,2,8,4096]{3,2,1,0:T(8,128)(2,1)}, u32[]{:S(2)}, u32[]{:S(2)}) %all-to-all-start.2) | async-done | bytes 4194336 | tf_op jit(solution)/shard_map/all_to_all | solution.py:78
  146.5 3.1 fusion.34
  149.6 3.1 multiply_convert_fusion.5
  152.8 4.2 fusion.55
  157.0 7.7 %all-to-all-start.3 = ((f32[32,8,4096]{2,1,0:T(8,128)}), f32[32,8,4096]{2,1,0:T(8,128)}, u32[]{:S(2)}, u32[]{:S(2)}) async-start(f32[32,8,4096]{2,1,0:T(8,128)} %fusion.55), calls=%async_computation.3 | async-start | bytes 8388608 | tf_op jit(solution)/shard_map/all_to_all | solution.py:44
  165.4 50.4 %all-to-all-done.3 = f32[32,8,4096]{2,1,0:T(8,128)} async-done(((f32[32,8,4096]{2,1,0:T(8,128)}), f32[32,8,4096]{2,1,0:T(8,128)}, u32[]{:S(2)}, u32[]{:S(2)}) %all-to-all-start.3) | async-done | bytes 4194336 | tf_op jit(solution)/shard_map/all_to_all | solution.py:44
  215.8 0.6 broadcast_in_dim.13
  216.4 10.2 %all-to-all-start.1 = ((s32[32,1,2]{2,1,0:T(1,128)}), s32[32,1,2]{2,1,0:T(1,128)S(1)}, u32[]{:S(2)}, u32[]{:S(2)}) async-start(s32[32,1,2]{2,1,0:T(1,128)} %broadcast_in_dim.13), calls=%async_computation.1 | async-start | bytes 32768 | tf_op jit(solution)/shard_map/all_to_all | solution.py:26
  226.7 2.4 reduce_sum.28
  229.1 4.6 all-to-all-done.1
  233.8 1.6 broadcast_in_dim.14
  235.3 4.8 all-to-all-start.4
  241.4 2.0 copy.42
  243.4 3.9 convert_bitcast_fusion
  247.3 6.5 %copy.39 = f32[4,3,28,8,1024]{4,3,0,2,1:T(8,128)} copy(f32[4,3,28,8,1024]{4,3,2,1,0:T(8,128)S(1)} %convert_bitcast_fusion) | data formatting | bytes 22020096 | tf_op jit(solution)/shard_map/convert_element_type | solution.py:67
  253.8 10.7 %all-to-all-done.4 = bf16[32,8,4096]{2,1,0:T(8,128)(2,1)} async-done(((bf16[32,8,4096]{2,1,0:T(8,128)(2,1)}), bf16[32,8,4096]{2,1,0:T(8,128)(2,1)}, u32[]{:S(2)}, u32[]{:S(2)}) %all-to-all-start.4) | async-done | bytes 2097184 | tf_op jit(solution)/shard_map/all_to_all | solution.py:26
  264.5 2.5 fusion.36
  267.1 2.4 fusion.17
  269.6 4.2 fusion.18
  273.8 3.6 fusion.16
  277.5 11.2 %fusion.65 = bf16[3,224,4096]{2,1,0:T(8,128)(2,1)S(1)} fusion(f32[3,224,4096]{2,1,0:T(8,128)S(1)} %bitcast.143, bf16[1,3,224,4096]{3,2,1,0:T(8,128)(2,1)S(1)} %bitcast.149, f32[1,224,4096]{2,1,0:T(8,128)S(1)} %fusion.16, f32[1,224,4096]{2,1,0:T(8,128)S(1)} %fusion.17, f32[1,224,4096]{2,1,0:T(8,128)S(1)} %fusion.18, bf16[1,3,224,4096]{3,2,1,0:T(8,128)(2,1)} %param.9, ...), kind=kLoop, calls=%fused_computation.94 | loop fusion | flops 52297728 | bytes 38535168 | tf_op jit(solution)/shard_map/convert_element_type | solution.py:81
  288.7 4.0 fusion.40
  292.7 2.4 multiply_convert_fusion.2
  295.2 2.2 fusion.27
  297.4 52.3 %all_to_all.37 = f32[32,8,4096]{2,1,0:T(8,128)} all-to-all(f32[32,8,4096]{2,1,0:T(8,128)S(1)} %fusion.27), channel_id=1, replica_groups=mesh['isl'=4,'fsdp'=32] {'fsdp'}, dimensions={0} | all-to-all | bytes 8388608 | tf_op jit(solution)/shard_map/all_to_all | solution.py:44
  349.7 2.4 reduce_sum.29
  352.2 1.6 broadcast_in_dim.15
  353.8 8.7 %all-to-all-start.6 = ((bf16[32,8,4096]{2,1,0:T(8,128)(2,1)}), bf16[32,8,4096]{2,1,0:T(8,128)(2,1)S(1)}, u32[]{:S(2)}, u32[]{:S(2)}) async-start(bf16[32,8,4096]{2,1,0:T(8,128)(2,1)} %broadcast_in_dim.15), calls=%async_computation.6 | async-start | bytes 4194304 | tf_op jit(solution)/shard_map/all_to_all | solution.py:26
  363.2 26.1 %all-to-all-done.6 = bf16[32,8,4096]{2,1,0:T(8,128)(2,1)S(1)} async-done(((bf16[32,8,4096]{2,1,0:T(8,128)(2,1)}), bf16[32,8,4096]{2,1,0:T(8,128)(2,1)S(1)}, u32[]{:S(2)}, u32[]{:S(2)}) %all-to-all-start.6) | async-done | bytes 2097184 | tf_op jit(solution)/shard_map/all_to_all | solution.py:26
  389.3 2.4 fusion.43
  391.8 4.2 fusion.14
  396.0 2.5 fusion.15
  398.5 2.6 fusion.13
  401.6 20.4 %fusion.12 = bf16[3,224,4096]{2,1,0:T(8,128)(2,1)} fusion(f32[3,224,4096]{2,1,0:T(8,128)S(1)} %bitcast.146, f32[1,224,4096]{2,1,0:T(8,128)} %fusion.13, f32[1,224,4096]{2,1,0:T(8,128)} %fusion.14, f32[1,224,4096]{2,1,0:T(8,128)S(1)} %fusion.15, f32[1,224,4096]{2,1,0:T(8,128)S(1)} %copy-done.5, f32[1,224,4096]{2,1,0:T(8,128)S(1)} %copy-done.3, ...), kind=kLoop, calls=%fused_computation.23 | loop fusion | flops 104595456 | bytes 49545216 | tf_op jit(solution)/shard_map/convert_element_type | solution.py:115
  422.0 63.1 %reduce-scatter.2.cloned.1.call-done = bf16[3,224,1024]{2,1,0:T(8,128)(2,1)} async-done(((bf16[3,224,4096]{2,1,0:T(8,128)(2,1)}), bf16[3,224,1024]{2,1,0:T(8,128)(2,1)}) %reduce-scatter.2.cloned.1.call-update) | async-done | bytes 1376272 | tf_op jit(solution)/shard_map/reduce_scatter | solution.py:114
  485.2 5.7 %multiply_subtract_fusion = (f32[3,224,1024]{2,1,0:T(8,128)}, f32[3,224,1024]{2,1,0:T(8,128)}) fusion(f32[3,224,1024]{2,1,0:T(8,128)S(1)} %copy-done.6, bf16[3,224,1024]{2,1,0:T(8,128)(2,1)} %reduce-scatter.2.cloned.1.call-done, f32[3,224,1024]{2,1,0:T(8,128)} %param.8), kind=kLoop, calls=%fused_computation.36 | loop fusion | flops 5505024 | bytes 12386304 | tf_op jit(solution)/shard_map/sub | solution.py:119
  (64 shorter events, 1.6 us)
Async XLA Ops:
  9.9 69.3 %copy-start.13 = (bf16[2,8,4096]{2,1,0:T(8,128)(2,1)S(1)}, bf16[2,8,4096]{2,1,0:T(8,128)(2,1)}, u32[]{:S(2)}) copy-start(bf16[2,8,4096]{2,1,0:T(8,128)(2,1)} %param.11) | copy-start | bytes 393220
  81.8 64.7 %all-to-all-start.2 = ((bf16[32,2,8,4096]{3,2,1,0:T(8,128)(2,1)}), bf16[32,2,8,4096]{3,2,1,0:T(8,128)(2,1)}, u32[]{:S(2)}, u32[]{:S(2)}) async-start(bf16[32,2,8,4096]{3,2,1,0:T(8,128)(2,1)} %stack.18), calls=%async_computation.2 | async-start | bytes 8388608 | tf_op jit(solution)/shard_map/all_to_all | solution.py:78
  98.2 5.1 %copy-start.9 = (bf16[1,224,4,1024]{3,1,0,2:T(8,128)(2,1)S(1)}, bf16[1,224,4,1024]{3,1,0,2:T(8,128)(2,1)}, u32[]{:S(2)}) copy-start(bf16[1,224,4,1024]{3,1,0,2:T(8,128)(2,1)} %get-tuple-element.6) | copy-start | bytes 5505028
  146.5 3.1 copy-start.10
  152.7 4.3 copy-start.11
  157.0 58.8 %all-to-all-start.3 = ((f32[32,8,4096]{2,1,0:T(8,128)}), f32[32,8,4096]{2,1,0:T(8,128)}, u32[]{:S(2)}, u32[]{:S(2)}) async-start(f32[32,8,4096]{2,1,0:T(8,128)} %fusion.55), calls=%async_computation.3 | async-start | bytes 8388608 | tf_op jit(solution)/shard_map/all_to_all | solution.py:44
  164.7 64.4 %copy-start.16 = (bf16[2,8,4096]{2,1,0:T(8,128)(2,1)S(1)}, bf16[2,8,4096]{2,1,0:T(8,128)(2,1)}, u32[]{:S(2)}) copy-start(bf16[2,8,4096]{2,1,0:T(8,128)(2,1)} %param.12) | copy-start | bytes 393220
  216.4 17.3 %all-to-all-start.1 = ((s32[32,1,2]{2,1,0:T(1,128)}), s32[32,1,2]{2,1,0:T(1,128)S(1)}, u32[]{:S(2)}, u32[]{:S(2)}) async-start(s32[32,1,2]{2,1,0:T(1,128)} %broadcast_in_dim.13), calls=%async_computation.1 | async-start | bytes 32768 | tf_op jit(solution)/shard_map/all_to_all | solution.py:26
  235.3 29.2 %all-to-all-start.4 = ((bf16[32,8,4096]{2,1,0:T(8,128)(2,1)}), bf16[32,8,4096]{2,1,0:T(8,128)(2,1)}, u32[]{:S(2)}, u32[]{:S(2)}) async-start(bf16[32,8,4096]{2,1,0:T(8,128)(2,1)} %broadcast_in_dim.14), calls=%async_computation.4 | async-start | bytes 4194304 | tf_op jit(solution)/shard_map/all_to_all | solution.py:26
  247.3 17.3 %copy-start.8 = (bf16[28,8,4,1024]{3,1,2,0:T(8,128)(2,1)S(1)}, bf16[28,8,4,1024]{3,1,2,0:T(8,128)(2,1)}, u32[]{:S(2)}) copy-start(bf16[28,8,4,1024]{3,1,2,0:T(8,128)(2,1)} %copy.42) | copy-start | bytes 5505028
  264.5 5.0 %copy-start.15 = (f32[256,224]{0,1:T(8,128)S(1)}, f32[256,224]{0,1:T(8,128)}, u32[]{:S(2)}) copy-start(f32[256,224]{0,1:T(8,128)} %get-tuple-element.10) | copy-start | bytes 688132
  264.5 12.9 %slice-start = ((s8[11010048]{0:T(1024)(128)(4,1)}), s8[4194304]{0:T(1024)(128)(4,1)S(1)}, s32[]{:S(2)}) async-start(s8[11010048]{0:T(1024)(128)(4,1)} %bitcast.141), calls=%async_computation.9 | async-start | bytes 8388608
  267.1 10.4 %slice-start.1 = ((s8[11010048]{0:T(1024)(128)(4,1)}), s8[4194304]{0:T(1024)(128)(4,1)S(1)}, s32[]{:S(2)}) async-start(s8[11010048]{0:T(1024)(128)(4,1)} %bitcast.141), calls=%async_computation.10 | async-start | bytes 8388608
  267.1 10.4 %slice-start.6 = ((s8[5505024]{0:T(1024)(128)(4,1)}), s8[4194304]{0:T(1024)(128)(4,1)S(1)}, s32[]{:S(2)}) async-start(s8[5505024]{0:T(1024)(128)(4,1)} %bitcast.148), calls=%async_computation.15 | async-start | bytes 8388608
  269.5 7.9 %copy-start.2 = (f32[1,224,4096]{2,1,0:T(8,128)}, f32[1,224,4096]{2,1,0:T(8,128)S(1)}, u32[]{:S(2)}) copy-start(f32[1,224,4096]{2,1,0:T(8,128)S(1)} %fusion.17) | copy-start | bytes 11010052
  269.6 4.2 copy-start.12
  269.6 7.9 %slice-start.2 = ((s8[11010048]{0:T(1024)(128)(4,1)}), s8[2621440]{0:T(1024)(128)(4,1)S(1)}, s32[]{:S(2)}) async-start(s8[11010048]{0:T(1024)(128)(4,1)} %bitcast.141), calls=%async_computation.11 | async-start | bytes 5242880
  269.6 7.9 %slice-start.7 = ((s8[5505024]{0:T(1024)(128)(4,1)}), s8[1310720]{0:T(1024)(128)(4,1)S(1)}, s32[]{:S(2)}) async-start(s8[5505024]{0:T(1024)(128)(4,1)} %bitcast.148), calls=%async_computation.16 | async-start | bytes 2621440
  273.8 14.9 %copy-start = (f32[1,224,4096]{2,1,0:T(8,128)}, f32[1,224,4096]{2,1,0:T(8,128)S(1)}, u32[]{:S(2)}) copy-start(f32[1,224,4096]{2,1,0:T(8,128)S(1)} %fusion.18) | copy-start | bytes 11010052
  277.4 11.3 %copy-start.4 = (f32[1,224,4096]{2,1,0:T(8,128)}, f32[1,224,4096]{2,1,0:T(8,128)S(1)}, u32[]{:S(2)}) copy-start(f32[1,224,4096]{2,1,0:T(8,128)S(1)} %fusion.16) | copy-start | bytes 11010052
  288.7 6.4 %copy-start.7 = (bf16[3,224,4096]{2,1,0:T(8,128)(2,1)}, bf16[3,224,4096]{2,1,0:T(8,128)(2,1)S(1)}, u32[]{:S(2)}) copy-start(bf16[3,224,4096]{2,1,0:T(8,128)(2,1)S(1)} %fusion.65) | copy-start | bytes 16515076
  349.7 2.4 copy-start.14
  349.7 2.5 copy-start.17
  353.8 35.5 %all-to-all-start.6 = ((bf16[32,8,4096]{2,1,0:T(8,128)(2,1)}), bf16[32,8,4096]{2,1,0:T(8,128)(2,1)S(1)}, u32[]{:S(2)}, u32[]{:S(2)}) async-start(bf16[32,8,4096]{2,1,0:T(8,128)(2,1)} %broadcast_in_dim.15), calls=%async_computation.6 | async-start | bytes 4194304 | tf_op jit(solution)/shard_map/all_to_all | solution.py:26
  362.5 122.7 %reduce-scatter.2.cloned.1.call-start = ((), (), s32[]{:S(2)}) async-start(), calls=%async_computation.8 | async-start | bytes 6881280 | tf_op jit(solution)/shard_map/reduce_scatter | solution.py:114
  389.3 11.7 %slice-start.3 = ((s8[11010048]{0:T(1024)(128)(4,1)}), s8[4194304]{0:T(1024)(128)(4,1)S(1)}, s32[]{:S(2)}) async-start(s8[11010048]{0:T(1024)(128)(4,1)} %bitcast.144), calls=%async_computation.12 | async-start | bytes 8388608
  391.7 9.3 %slice-start.4 = ((s8[11010048]{0:T(1024)(128)(4,1)}), s8[4194304]{0:T(1024)(128)(4,1)S(1)}, s32[]{:S(2)}) async-start(s8[11010048]{0:T(1024)(128)(4,1)} %bitcast.144), calls=%async_computation.13 | async-start | bytes 8388608
  391.8 9.3 %copy-start.5 = (f32[1,224,4096]{2,1,0:T(8,128)S(1)}, f32[1,224,4096]{2,1,0:T(8,128)}, u32[]{:S(2)}) copy-start(f32[1,224,4096]{2,1,0:T(8,128)} %copy-done.4) | copy-start | bytes 11010052
  396.0 5.1 %slice-start.5 = ((s8[11010048]{0:T(1024)(128)(4,1)}), s8[2621440]{0:T(1024)(128)(4,1)S(1)}, s32[]{:S(2)}) async-start(s8[11010048]{0:T(1024)(128)(4,1)} %bitcast.144), calls=%async_computation.14 | async-start | bytes 5242880
  396.0 5.1 %copy-start.3 = (f32[1,224,4096]{2,1,0:T(8,128)S(1)}, f32[1,224,4096]{2,1,0:T(8,128)}, u32[]{:S(2)}) copy-start(f32[1,224,4096]{2,1,0:T(8,128)} %copy-done.2) | copy-start | bytes 11010052
  398.5 3.1 copy-start.1
  422.0 63.2 %copy-start.6 = (f32[3,224,1024]{2,1,0:T(8,128)S(1)}, f32[3,224,1024]{2,1,0:T(8,128)}, u32[]{:S(2)}) copy-start(f32[3,224,1024]{2,1,0:T(8,128)} %param.7) | copy-start | bytes 8257540
Sparse Core Ops, SparseCore 0:
  422.1 62.9 reduce-scatter.1
